TPU v7x, 32 devices: a whole 2x2x4 slice. The times are simulated.
32 devices in a mesh: shard: 32 (over z, y, x, core).
Axes of the slice: x: 2, y: 2, z: 4, core: 2. Of those that a mesh axis runs over, the one named last changes fastest.
Arguments:
- data_t: bfloat16 [8192, 8192], P('shard'), may hold values from -0.125 to 0.125
- labels: int32 [8192], replicated, may hold values from -1 to 1, as said below
- sample_weight: float32 [8192], replicated, may hold values from 0.1 to 4
- w_start: float32 [8192], P('shard'), may hold values from -10 to 10
- alpha_start: float32 [8192], P('shard'), may hold values from 0 to 1
- visit_order: int32 [64, 128], P('shard'), may hold values from 0 to 127, each once within a row
Outputs:
- weights_out: float32 [8192], P('shard')
- alpha_final: float32 [8192], P('shard')
- objective: float32 [], replicated
Inputs may be any that keep to these rules, and one draw needn't show every extreme that they name: `labels`: each label is -1 or +1. `visit_order`: each row is a permutation of 0 to 127.
All inputs are finite; a program needn't handle non-finite values.
Results may differ from a plain program's by a relative error of at most 0.0047.
Values may be sent and summed in bfloat16 or wider, within the bound.
A program may use at most 64 MiB of HBM per device.

v0:
```python
import jax
import jax.numpy as jnp
from jax import lax
from jax.sharding import PartitionSpec as P

GROUP = 16


def sweep_rows(gram_block, label_rows, bound_rows, alpha_rows, margin_rows, visit_rows):
    gram_perm = gram_block[visit_rows][:, visit_rows]
    label_perm = label_rows[visit_rows]
    bound_perm = bound_rows[visit_rows]
    alpha_perm = alpha_rows[visit_rows]
    margin_perm = margin_rows[visit_rows]
    diag_perm = jnp.diagonal(gram_perm) + 1e-06

    def update_group(group_index, state_pair):
        alpha_now, margin_now = state_pair
        first_row = jnp.asarray(group_index * GROUP).astype(jnp.int32)
        group_alpha = lax.dynamic_slice_in_dim(alpha_now, first_row, GROUP)
        group_label = lax.dynamic_slice_in_dim(label_perm, first_row, GROUP)
        group_margin = lax.dynamic_slice_in_dim(margin_now, first_row, GROUP)
        group_diag = lax.dynamic_slice_in_dim(diag_perm, first_row, GROUP)
        group_bound = lax.dynamic_slice_in_dim(bound_perm, first_row, GROUP)
        fresh_alpha = jnp.clip(
            group_alpha + (1.0 - group_label * group_margin) / (2.0 * group_diag), 0.0, group_bound
        )
        change = fresh_alpha - group_alpha
        columns = lax.dynamic_slice_in_dim(gram_perm, first_row, GROUP, 1)
        margin_now = margin_now + 2.0 * jnp.dot(
            columns, group_label * change, precision=lax.Precision.HIGHEST
        )
        alpha_now = lax.dynamic_update_slice_in_dim(alpha_now, fresh_alpha, first_row, 0)
        return (alpha_now, margin_now)

    alpha_perm, margin_perm = lax.fori_loop(
        0, alpha_rows.shape[0] // GROUP, update_group, (alpha_perm, margin_perm)
    )
    return jnp.zeros_like(alpha_rows).at[visit_rows].set(alpha_perm)


def body(data_t, labels, sample_weight, w_start, alpha_start, visit_order):
    device_index = lax.axis_index("shard")
    devices = lax.axis_size("shard")
    local_feat = data_t.shape[0]
    samples = labels.shape[0]
    row_count = alpha_start.shape[0]
    features = local_feat * devices
    label_sign = labels.astype(jnp.float32)
    row_first = device_index * row_count
    own_signs = lax.dynamic_slice_in_dim(label_sign, row_first, row_count)
    own_bound = lax.dynamic_slice_in_dim(sample_weight, row_first, row_count)
    relaid = lax.all_to_all(data_t, "shard", split_axis=1, concat_axis=0, tiled=True)
    start_part = jnp.dot(w_start.astype(jnp.bfloat16), data_t, preferred_element_type=jnp.float32)
    start_margin = lax.psum(start_part, "shard")
    weighted = (
        sample_weight * label_sign * jnp.maximum(0.0, 1.0 - label_sign * start_margin)
    ).astype(jnp.bfloat16)
    ascent = jnp.dot(data_t, weighted, preferred_element_type=jnp.float32)
    column_sq = jnp.einsum("fs,fs->f", data_t, data_t, preferred_element_type=jnp.float32)
    scale_col = column_sq / samples + 1e-06
    stepped = w_start + ascent / (samples * scale_col)
    thresh = 1.0 / (4.0 * features * scale_col)
    primal = stepped - jnp.clip(stepped, -thresh, thresh)
    model_part = jnp.dot(primal.astype(jnp.bfloat16), data_t, preferred_element_type=jnp.float32)
    penalty_part = jnp.sum(jnp.abs(primal)) / (4.0 * features)
    own_margin = lax.psum_scatter(model_part, "shard", scatter_dimension=0, tiled=True)
    loss_part = jnp.sum(own_bound * jnp.square(jnp.maximum(0.0, 1.0 - own_signs * own_margin))) / (
        2.0 * samples
    )
    loss_total, penalty = lax.psum((loss_part, penalty_part), "shard")
    objective = loss_total + penalty
    gram_block = lax.dot_general(
        relaid, relaid, (((0,), (0,)), ((), ())), preferred_element_type=jnp.float32
    )
    block_count = visit_order.shape[0]
    visit_rows = (
        visit_order + (jnp.arange(block_count, dtype=jnp.int32) * visit_order.shape[1])[:, None]
    ).reshape(row_count)
    alpha_zero = own_bound * alpha_start
    alpha_one = sweep_rows(gram_block, own_signs, own_bound, alpha_zero, own_margin, visit_rows)
    change_one = (own_signs * (alpha_one - alpha_zero)).astype(jnp.bfloat16)
    update_part = jnp.dot(relaid, change_one, preferred_element_type=jnp.float32) * (2.0 / devices)
    update_one = lax.psum(update_part, "shard")
    second_margin = own_margin + jnp.dot(
        update_one.astype(jnp.bfloat16), relaid, preferred_element_type=jnp.float32
    )
    alpha_two = sweep_rows(gram_block, own_signs, own_bound, alpha_one, second_margin, visit_rows)
    change_two = (own_signs * (alpha_two - alpha_one)).astype(jnp.bfloat16)
    second_part = jnp.dot(relaid, change_two, preferred_element_type=jnp.float32) * (2.0 / devices)
    feat_first = device_index * local_feat
    update_two = lax.psum(second_part, "shard")
    own_two = lax.dynamic_slice_in_dim(update_two, feat_first, local_feat)
    own_one = lax.dynamic_slice_in_dim(update_one, feat_first, local_feat)
    return (primal + own_one + own_two, alpha_two, objective)


def solution(mesh):
    placed = (P("shard", None), P(), P(), P("shard"), P("shard"), P("shard", None))
    return jax.shard_map(
        body, mesh=mesh, in_specs=placed, out_specs=(P("shard"), P("shard"), P()), check_vma=False
    )
```

profile of v0, /device:TPU:14, one launch (start us, length us, event | category | flops | bytes accessed | tf_op | source)
XLA Modules:
  0.0 315.5 jit_solution(12440864550533348112)
XLA Ops:
  0.6 6.4 %copy.19 = bf16[256,8192]{0,1:T(8,128)(2,1)} copy(bf16[256,8192]{1,0:T(8,128)(2,1)} %param.10) | data formatting | bytes 8388608 | tf_op args[0]
  7.0 6.4 %copy.20 = bf16[256,32,256]{2,0,1:T(8,128)(2,1)} copy(bf16[256,32,256]{0,2,1:T(8,128)(2,1)} %bitcast.48) | data formatting | bytes 8388608 | tf_op jit(solution)/shard_map/all_to_all | solution.py:53
  13.4 6.0 %all-to-all-start = ((bf16[256,32,256]{2,0,1:T(8,128)(2,1)}), bf16[256,32,256]{2,0,1:T(8,128)(2,1)}, u32[]{:S(2)}, u32[]{:S(2)}) async-start(bf16[256,32,256]{2,0,1:T(8,128)(2,1)} %copy.20), calls=%async_computation | async-start | bytes 8388608 | tf_op jit(solution)/shard_map/all_to_all | solution.py:53
  19.5 2.8 fusion.28
  22.4 109.1 %psum.35 = f32[8192]{0:T(1024)S(1)} all-reduce(f32[8192]{0:T(1024)S(1)} %bitcast.53), channel_id=1, replica_groups=mesh['shard'=32] {'shard'}, use_global_device_ids=true, to_apply=%region_0.0 | all-reduce | flops 8192 | bytes 65536 | tf_op jit(solution)/shard_map/psum | solution.py:55
  131.5 3.5 %fusion.29 = f32[1,256]{1,0:T(1,128)S(1)} fusion(bf16[8192,1]{0,1:T(2,128)(2,1)S(1)} %reshape.137, bf16[256,8192]{1,0:T(8,128)(2,1)} %param.10), kind=kOutput, calls=%fused_computation.58 | convolution fusion | flops 4194304 | bytes 4211712 | tf_op jit(solution)/shard_map/dot_general | solution.py:59
  135.1 0.9 fusion.16
  136.0 0.6 abs_reduce_fusion
  136.6 2.8 fusion.30
  139.5 42.1 %all-reduce = f32[8192]{0:T(1024)S(1)} all-reduce(f32[8192]{0:T(1024)S(1)} %bitcast.54), channel_id=2, replica_groups=mesh['shard'=32] {'shard'}, use_global_device_ids=true, to_apply=%region_1.2.clone | all-reduce | flops 8192 | bytes 65536
  181.6 0.7 multiply_reduce_fusion
  182.3 1.9 gather_fusion.3
  184.3 1.9 gather_fusion.2
  186.3 1.9 gather_fusion
  188.2 1.9 gather_fusion.1
  191.5 4.7 %fusion.19 = f32[256,256]{1,0:T(8,128)S(1)} fusion(bf16[256,32,256]{2,0,1:T(8,128)(2,1)} %all-to-all-done), kind=kOutput, calls=%fused_computation.35 | convolution fusion | flops 1073741824 | bytes 4456448 | tf_op jit(solution)/shard_map/dot_general | solution.py:73
  196.2 1.0 gather_fusion.4
  197.3 1.0 gather_fusion.5
  198.5 2.4 gather_fusion.6
  200.8 8.5 %while.30 = (s32[]{:T(128)}, f32[256]{0:T(256)S(1)}, f32[256]{0:T(256)S(1)}, f32[256]{0:T(256)S(1)}, f32[256]{0:T(256)S(1)}, /*index=5*/f32[256]{0:T(256)S(1)}, ...) while((s32[]{:T(128)}, f32[256]{0:T(256)S(1)}, f32[256]{0:T(256)S(1)}, ...), condition=%wide.region_3.4_spmd, body=%wide.region_2.3_spmd.sunk | while | flops 49814 | bytes 145567 | solution.py:36
  200.9 0.2 fusion.56
  201.1 0.2 fusion.57
  201.6 0.2 fusion.57
  202.1 0.2 fusion.57
  202.6 0.2 fusion.57
  203.2 0.2 fusion.57
  203.7 0.2 fusion.57
  204.2 0.2 fusion.57
  204.8 0.2 fusion.57
  205.3 0.2 fusion.57
  205.8 0.2 fusion.57
  206.4 0.2 fusion.57
  206.9 0.2 fusion.57
  207.4 0.2 fusion.57
  207.9 0.2 fusion.57
  208.5 0.2 fusion.57
  209.0 0.2 fusion.57
  209.3 1.4 scatter_custom_fusion
  210.7 1.9 gather_fusion.7
  212.7 3.4 %fusion.31 = f32[1,8192]{1,0:T(1,128)S(1)} fusion(bf16[256,1]{0,1:T(2,128)(2,1)S(1)} %reshape.144, bf16[8192,256]{1,0:T(8,128)(2,1)} %bitcast.14), kind=kOutput, calls=%fused_computation.60 | convolution fusion | flops 4194304 | bytes 4227584 | tf_op jit(solution)/shard_map/dot_general | solution.py:83
  216.1 38.4 %psum.36 = f32[8192]{0:T(1024)S(1)} all-reduce(f32[8192]{0:T(1024)S(1)} %broadcast_multiply_fusion.1), channel_id=1, replica_groups=mesh['shard'=32] {'shard'}, use_global_device_ids=true, to_apply=%region_5.6 | all-reduce | flops 8192 | bytes 65536 | tf_op jit(solution)/shard_map/psum | solution.py:84
  254.5 2.8 fusion.32
  257.4 2.0 gather_fusion.8
  259.3 8.5 %while.31 = (s32[]{:T(128)}, f32[256]{0:T(256)S(1)}, f32[256]{0:T(256)S(1)}, f32[256]{0:T(256)S(1)}, f32[256]{0:T(256)S(1)}, /*index=5*/f32[256]{0:T(256)S(1)}, ...) while((s32[]{:T(128)}, f32[256]{0:T(256)S(1)}, f32[256]{0:T(256)S(1)}, ...), condition=%wide.region_7.8_spmd, body=%wide.region_6.7_spmd.sunk | while | flops 49814 | bytes 145567 | solution.py:36
  259.5 0.2 fusion.61
  260.0 0.2 fusion.61
  260.6 0.2 fusion.61
  261.1 0.2 fusion.61
  261.6 0.2 fusion.61
  262.2 0.2 fusion.61
  262.7 0.2 fusion.61
  263.2 0.2 fusion.61
  263.8 0.2 fusion.61
  264.3 0.2 fusion.61
  264.8 0.2 fusion.61
  265.3 0.2 fusion.61
  265.9 0.2 fusion.61
  266.4 0.2 fusion.61
  266.9 0.2 fusion.61
  267.5 0.2 fusion.61
  267.8 1.4 scatter_custom_fusion.1
  269.2 3.4 %fusion.33 = f32[1,8192]{1,0:T(1,128)S(1)} fusion(bf16[256,1]{0,1:T(2,128)(2,1)S(1)} %reshape.148, bf16[8192,256]{1,0:T(8,128)(2,1)} %bitcast.14), kind=kOutput, calls=%fused_computation.62 | convolution fusion | flops 4194304 | bytes 4227584 | tf_op jit(solution)/shard_map/dot_general | solution.py:90
  272.6 42.2 %all-reduce.1 = (f32[8192]{0:T(1024)S(1)}, f32[]{:T(128)}) all-reduce(f32[8192]{0:T(1024)S(1)} %broadcast_multiply_fusion, f32[]{:T(128)S(6)} %add.173), channel_id=1, replica_groups=mesh['shard'=32] {'shard'}, use_global_device_ids=true, to_apply=%region_9.10 | all-reduce | flops 8193 | bytes 65544 | tf_op jit(solution)/shard_map/psum | solution.py:92
  314.8 0.6 dynamic-slice_add_fusion
  (167 shorter events, 7.9 us)
Async XLA Ops:
  13.4 6.1 %copy-start.6 = (f32[256]{0:T(256)S(1)}, f32[256]{0:T(256)}, u32[]{:S(2)}) copy-start(f32[256]{0:T(256)} %param.13) | copy-start | bytes 3076
  13.4 6.1 %copy-start.1 = (s32[8192]{0:T(1024)S(1)}, s32[8192]{0:T(1024)}, u32[]{:S(2)}) copy-start(s32[8192]{0:T(1024)} %param.11) | copy-start | bytes 98308
  13.4 178.0 %all-to-all-start = ((bf16[256,32,256]{2,0,1:T(8,128)(2,1)}), bf16[256,32,256]{2,0,1:T(8,128)(2,1)}, u32[]{:S(2)}, u32[]{:S(2)}) async-start(bf16[256,32,256]{2,0,1:T(8,128)(2,1)} %copy.20), calls=%async_computation | async-start | bytes 8388608 | tf_op jit(solution)/shard_map/all_to_all | solution.py:53
  19.5 112.0 %copy-start.2 = (f32[8192]{0:T(1024)S(1)}, f32[8192]{0:T(1024)}, u32[]{:S(2)}) copy-start(f32[8192]{0:T(1024)} %param.12) | copy-start | bytes 98308
  131.5 3.6 %copy-start = (bf16[256,8192]{1,0:T(8,128)(2,1)S(1)}, bf16[256,8192]{1,0:T(8,128)(2,1)}, u32[]{:S(2)}) copy-start(bf16[256,8192]{1,0:T(8,128)(2,1)} %param.10) | copy-start | bytes 12582916
  135.1 47.2 %copy-start.5 = (s32[2,128]{1,0:T(2,128)S(1)}, s32[2,128]{1,0:T(2,128)}, u32[]{:S(2)}) copy-start(s32[2,128]{1,0:T(2,128)} %param.15) | copy-start | bytes 3076
  136.0 50.2 %copy-start.3 = (f32[256]{0:T(256)S(1)}, f32[256]{0:T(256)}, u32[]{:S(2)}) copy-start(f32[256]{0:T(256)} %param.14) | copy-start | bytes 3076
  269.2 46.3 %copy-start.4 = (f32[256]{0:T(256)}, f32[256]{0:T(256)S(1)}, u32[]{:S(2)}) copy-start(f32[256]{0:T(256)S(1)} %scatter_custom_fusion.1) | copy-start | bytes 3076
where the time goes:
time: 316 us; the launch traced here: 315 us
  blocking collectives  232 us (73%)
  local copies, waits for them, and re-layouts  32.1 us (10%)
  matrix products  31.5 us (10%)
  other arithmetic  10.4 us (3%)
  starting transfers between devices  6.02 us (2%)
    psum x1, blocking collectives, body(): start_margin = lax.psum(start_part, 'shard')  109 us
    psum x1, blocking collectives, body(): update_two = lax.psum(second_part, 'shard')  42.2 us
    unnamed x1, blocking collectives  42.1 us
    psum x1, blocking collectives, body(): update_one = lax.psum(update_part, 'shard')  38.4 us
    dot_general x32, matrix products, update_group(): jnp.dot(columns, group_label * change, precision=lax.Precision.HIGHEST)  7.97 us
    unnamed x15, local copies, waits for them, and re-layouts  6.44 us
    all_to_all x1, local copies, waits for them, and re-layouts, body(): lax.all_to_all(data_t, 'shard', split_axis=1, concat_axis=0, tiled=True)  6.41 us
  transfers between devices with their start and end apart: 1, of which 0 were waited for; matrix products, arithmetic and copies ran while one was open for 6% of the time, Pallas kernels for 0%

commit v1 on v0

--- a/solution.py
+++ b/solution.py
@@ -89,7 +89,7 @@
     change_two = (own_signs * (alpha_two - alpha_one)).astype(jnp.bfloat16)
     second_part = jnp.dot(relaid, change_two, preferred_element_type=jnp.float32) * (2.0 / devices)
     feat_first = device_index * local_feat
-    update_two = lax.psum(second_part, "shard")
+    update_two = jnp.sum(lax.all_gather(second_part, "shard"), axis=0)
     own_two = lax.dynamic_slice_in_dim(update_two, feat_first, local_feat)
     own_one = lax.dynamic_slice_in_dim(update_one, feat_first, local_feat)
     return (primal + own_one + own_two, alpha_two, objective)

time: 316 us -> 347 us (1.098)
  waiting for transfers between devices: 0.01 us -> 54.5 us
  blocking collectives: 232 us -> 190 us
  between operations: 2.28 us -> 15.7 us
    all_gather x0 -> x1, waiting for transfers between devices: none -> 54.5 us  [body(): update_two = jnp.sum(lax.all_gather(second_part, 'shard'), axis=0)]
    psum x1 -> x0, blocking collectives: 42.2 us -> none  [body(): update_two = lax.psum(second_part, 'shard')]
  transfers between devices with their start and end apart: 1 -> 2, of which waited for: 0 -> 1; matrix products, arithmetic and copies ran while one was open for 6% -> 6% of each run, Pallas kernels for 0% -> 0%
where the time goes in v1:
time: 347 us; the launch traced here: 344 us
  blocking collectives  190 us (55%)
  waiting for transfers between devices  54.5 us (16%)
  local copies, waits for them, and re-layouts  33.7 us (10%)
  matrix products  31.5 us (9%)
  between operations  15.7 us (5%)
  other arithmetic  11.2 us (3%)
  starting transfers between devices  6.06 us (2%)
    psum x1, blocking collectives, body(): start_margin = lax.psum(start_part, 'shard')  109 us
    all_gather x1, waiting for transfers between devices, body(): update_two = jnp.sum(lax.all_gather(second_part, 'shard'), axis=0)  54.5 us
    unnamed x1, blocking collectives  42.1 us
    psum x1, blocking collectives, body(): update_one = lax.psum(update_part, 'shard')  38.5 us
    dot_general x32, matrix products, update_group(): jnp.dot(columns, group_label * change, precision=lax.Precision.HIGHEST)  7.97 us
  transfers between devices with their start and end apart: 2, of which 1 were waited for; matrix products, arithmetic and copies ran while one was open for 6% of the time, Pallas kernels for 0%

profile of v1, /device:TPU:14, one launch (start us, length us, event | category | flops | bytes accessed | tf_op | source)
XLA Modules:
  0.0 343.6 jit_solution(7898161168368959883)
XLA Ops:
  7.2 6.4 %copy.25 = bf16[256,8192]{0,1:T(8,128)(2,1)} copy(bf16[256,8192]{1,0:T(8,128)(2,1)} %param.10) | data formatting | bytes 8388608 | tf_op args[0]
  13.6 6.4 %copy.26 = bf16[256,32,256]{2,0,1:T(8,128)(2,1)} copy(bf16[256,32,256]{0,2,1:T(8,128)(2,1)} %bitcast.48) | data formatting | bytes 8388608 | tf_op jit(solution)/shard_map/all_to_all | solution.py:53
  20.0 6.0 %all-to-all-start = ((bf16[256,32,256]{2,0,1:T(8,128)(2,1)}), bf16[256,32,256]{2,0,1:T(8,128)(2,1)}, u32[]{:S(2)}, u32[]{:S(2)}) async-start(bf16[256,32,256]{2,0,1:T(8,128)(2,1)} %copy.26), calls=%async_computation | async-start | bytes 8388608 | tf_op jit(solution)/shard_map/all_to_all | solution.py:53
  26.1 2.8 fusion.28
  29.0 109.0 %psum.28 = f32[8192]{0:T(1024)S(1)} all-reduce(f32[8192]{0:T(1024)S(1)} %bitcast.53), channel_id=1, replica_groups=mesh['shard'=32] {'shard'}, use_global_device_ids=true, to_apply=%region_0.0 | all-reduce | flops 8192 | bytes 65536 | tf_op jit(solution)/shard_map/psum | solution.py:55
  138.1 3.5 %fusion.29 = f32[1,256]{1,0:T(1,128)S(1)} fusion(bf16[8192,1]{0,1:T(2,128)(2,1)S(1)} %reshape.138, bf16[256,8192]{1,0:T(8,128)(2,1)} %param.10), kind=kOutput, calls=%fused_computation.58 | convolution fusion | flops 4194304 | bytes 4211712 | tf_op jit(solution)/shard_map/dot_general | solution.py:59
  141.6 0.9 fusion.16
  142.5 0.6 abs_reduce_fusion
  143.2 2.8 fusion.30
  146.0 42.1 %all-reduce = f32[8192]{0:T(1024)S(1)} all-reduce(f32[8192]{0:T(1024)S(1)} %bitcast.54), channel_id=3, replica_groups=mesh['shard'=32] {'shard'}, use_global_device_ids=true, to_apply=%region_1.2.clone | all-reduce | flops 8192 | bytes 65536
  188.1 0.7 multiply_reduce_fusion
  188.9 1.9 gather_fusion.3
  190.8 1.9 gather_fusion.2
  192.8 1.9 gather_fusion
  194.8 1.9 gather_fusion.1
  198.0 4.7 %fusion.19 = f32[256,256]{1,0:T(8,128)S(1)} fusion(bf16[256,32,256]{2,0,1:T(8,128)(2,1)} %all-to-all-done), kind=kOutput, calls=%fused_computation.35 | convolution fusion | flops 1073741824 | bytes 4456448 | tf_op jit(solution)/shard_map/dot_general | solution.py:73
  202.8 1.0 gather_fusion.4
  203.9 1.0 gather_fusion.5
  205.0 2.4 gather_fusion.6
  207.4 8.5 %while.30 = (s32[]{:T(128)}, f32[256]{0:T(256)S(1)}, f32[256]{0:T(256)S(1)}, f32[256]{0:T(256)S(1)}, f32[256]{0:T(256)S(1)}, /*index=5*/f32[256]{0:T(256)S(1)}, ...) while((s32[]{:T(128)}, f32[256]{0:T(256)S(1)}, f32[256]{0:T(256)S(1)}, ...), condition=%wide.region_3.4_spmd, body=%wide.region_2.3_spmd.sunk | while | flops 49814 | bytes 145567 | solution.py:36
  207.6 0.2 fusion.57
  208.1 0.2 fusion.57
  208.7 0.2 fusion.57
  209.2 0.2 fusion.57
  209.7 0.2 fusion.57
  210.3 0.2 fusion.57
  210.8 0.2 fusion.57
  211.3 0.2 fusion.57
  211.9 0.2 fusion.57
  212.4 0.2 fusion.57
  212.9 0.2 fusion.57
  213.4 0.2 fusion.57
  214.0 0.2 fusion.57
  214.5 0.2 fusion.57
  215.0 0.2 fusion.57
  215.6 0.2 fusion.57
  215.9 1.6 scatter_custom_fusion
  217.5 1.9 gather_fusion.7
  219.5 3.4 fusion.31
  222.8 38.5 %all-reduce.1 = (f32[8192]{0:T(1024)S(1)}, f32[]{:T(128)}) all-reduce(f32[8192]{0:T(1024)S(1)} %broadcast_multiply_fusion.1, f32[]{:T(128)S(6)} %add.171), channel_id=1, replica_groups=mesh['shard'=32] {'shard'}, use_global_device_ids=true, to_apply=%region_5.6 | all-reduce | flops 8193 | bytes 65544 | tf_op jit(solution)/shard_map/psum | solution.py:84
  261.3 2.8 fusion.32
  264.2 2.0 gather_fusion.8
  266.1 8.5 %while.31 = (s32[]{:T(128)}, f32[256]{0:T(256)S(1)}, f32[256]{0:T(256)S(1)}, f32[256]{0:T(256)S(1)}, f32[256]{0:T(256)S(1)}, /*index=5*/f32[256]{0:T(256)S(1)}, ...) while((s32[]{:T(128)}, f32[256]{0:T(256)S(1)}, f32[256]{0:T(256)S(1)}, ...), condition=%wide.region_7.8_spmd, body=%wide.region_6.7_spmd.sunk | while | flops 49814 | bytes 145567 | solution.py:36
  266.4 0.2 fusion.61
  266.9 0.2 fusion.61
  267.4 0.2 fusion.61
  267.9 0.2 fusion.61
  268.5 0.2 fusion.61
  269.0 0.2 fusion.61
  269.5 0.2 fusion.61
  270.1 0.2 fusion.61
  270.6 0.2 fusion.61
  271.1 0.2 fusion.61
  271.7 0.2 fusion.61
  272.2 0.2 fusion.61
  272.7 0.2 fusion.61
  273.3 0.2 fusion.61
  273.8 0.2 fusion.61
  274.7 1.4 scatter_custom_fusion.1
  276.1 3.4 fusion.33
  279.5 0.6 broadcast_multiply_fusion
  280.1 54.5 %all-gather.3.cloned.1.call-done = f32[262144]{0:T(1024)} async-done(((f32[8192]{0:T(1024)}), f32[262144]{0:T(1024)}) %all-gather.3.cloned.1.call-update) | async-done | bytes 1048592 | tf_op jit(solution)/shard_map/all_gather | solution.py:92
  334.6 1.4 reshape.131
  336.1 0.6 dynamic-slice_add_fusion
  (171 shorter events, 8.5 us)
Async XLA Ops:
  20.0 6.1 %copy-start.6 = (f32[256]{0:T(256)S(1)}, f32[256]{0:T(256)}, u32[]{:S(2)}) copy-start(f32[256]{0:T(256)} %param.13) | copy-start | bytes 3076
  20.0 6.1 %copy-start.1 = (s32[8192]{0:T(1024)S(1)}, s32[8192]{0:T(1024)}, u32[]{:S(2)}) copy-start(s32[8192]{0:T(1024)} %param.11) | copy-start | bytes 98308
  20.0 178.1 %all-to-all-start = ((bf16[256,32,256]{2,0,1:T(8,128)(2,1)}), bf16[256,32,256]{2,0,1:T(8,128)(2,1)}, u32[]{:S(2)}, u32[]{:S(2)}) async-start(bf16[256,32,256]{2,0,1:T(8,128)(2,1)} %copy.26), calls=%async_computation | async-start | bytes 8388608 | tf_op jit(solution)/shard_map/all_to_all | solution.py:53
  26.0 112.0 %copy-start.2 = (f32[8192]{0:T(1024)S(1)}, f32[8192]{0:T(1024)}, u32[]{:S(2)}) copy-start(f32[8192]{0:T(1024)} %param.12) | copy-start | bytes 98308
  26.0 308.6 %all-gather.3.cloned.1.call-start = ((), (), s32[]{:S(2)}) async-start(), calls=%async_computation.1 | async-start | bytes 1081344 | tf_op jit(solution)/shard_map/all_gather | solution.py:92
  138.0 3.6 %copy-start = (bf16[256,8192]{1,0:T(8,128)(2,1)S(1)}, bf16[256,8192]{1,0:T(8,128)(2,1)}, u32[]{:S(2)}) copy-start(bf16[256,8192]{1,0:T(8,128)(2,1)} %param.10) | copy-start | bytes 12582916
  141.6 47.2 %copy-start.5 = (s32[2,128]{1,0:T(2,128)S(1)}, s32[2,128]{1,0:T(2,128)}, u32[]{:S(2)}) copy-start(s32[2,128]{1,0:T(2,128)} %param.15) | copy-start | bytes 3076
  142.5 50.2 %copy-start.3 = (f32[256]{0:T(256)S(1)}, f32[256]{0:T(256)}, u32[]{:S(2)}) copy-start(f32[256]{0:T(256)} %param.14) | copy-start | bytes 3076
  276.1 60.7 %copy-start.4 = (f32[256]{0:T(256)}, f32[256]{0:T(256)S(1)}, u32[]{:S(2)}) copy-start(f32[256]{0:T(256)S(1)} %scatter_custom_fusion.1) | copy-start | bytes 3076
Sparse Core Ops, SparseCore 0:
  280.2 54.3 all-gather.2
